TPU v7x, 32 devices: a whole 2x2x4 slice. The times are simulated.
32 devices in a mesh: gx: 4 (over z), gy: 4 (over x, core), gz: 2 (over y).
Axes of the slice: x: 2, y: 2, z: 4, core: 2. Of those that a mesh axis runs over, the one named last changes fastest.
Arguments:
- populations: float32 [19, 16, 32, 512], P(None, 'gz', 'gx', 'gy'), may hold values from 0 to 1, as said below
- omega: float32 [16, 32, 512], P('gz', 'gx', 'gy'), may hold values from 0.8 to 1.7
- obstacle: int32 [16, 32, 512], P('gz', 'gx', 'gy'), may hold values 0 or 1
Outputs:
- lifted: float32 [19, 16, 32, 512], P(None, 'gz', 'gx', 'gy')
- diagnostics: float32 [5], replicated
Inputs may be any that keep to these rules, and one draw needn't show every extreme that they name: `populations`: every population lies between 0.3 and 1.7 times its lattice weight.
All inputs are finite; a program needn't handle non-finite values. No bound on the sum of `obstacle` on one device may be relied on, other than what follows from the above.
Results may differ from a plain program's by a relative error of at most 0.0001.
Values sent between devices are 32-bit elements; how exact they have to be, the bound alone decides.
A program may use at most 128 MiB of HBM per device.

v0:
```python
import jax
import jax.numpy as jnp
from jax import lax
from jax.sharding import PartitionSpec as P

STEPS = 4
JUMP = 2
lattice = [
    (0, 0, 0),
    (1, 0, 0),
    (-1, 0, 0),
    (0, 1, 0),
    (0, -1, 0),
    (0, 0, 1),
    (0, 0, -1),
    (1, 1, 0),
    (-1, -1, 0),
    (1, -1, 0),
    (-1, 1, 0),
    (1, 0, 1),
    (-1, 0, -1),
    (1, 0, -1),
    (-1, 0, 1),
    (0, 1, 1),
    (0, -1, -1),
    (0, 1, -1),
    (0, -1, 1),
]
weights = [1.0 / 3.0] + [1.0 / 18.0] * 6 + [1.0 / 36.0] * 12
opposite = [0, 2, 1, 4, 3, 6, 5, 8, 7, 10, 9, 12, 11, 14, 13, 16, 15, 18, 17]
limiter = 25.0


def extended(x, sides, width):
    for axis, dim in sides:
        size, length = (lax.axis_size(axis), x.shape[dim])
        up = [(i, (i + 1) % size) for i in range(size)]
        down = [(j, i) for i, j in up]
        last = lax.slice_in_dim(x, length - width, length, axis=dim)
        first = lax.slice_in_dim(x, 0, width, axis=dim)
        before = lax.ppermute(last, axis, up)
        after = lax.ppermute(first, axis, down)
        x = jnp.concatenate([before, x, after], axis=dim)
    return x


def moments(f):
    rho = jnp.sum(f, axis=0)
    comps = []
    for axis_pick in range(3):
        total = jnp.zeros_like(rho)
        for index in range(19):
            comp = lattice[index][axis_pick]
            if comp != 0:
                total = total + comp * f[index]
        comps.append(total)
    return (rho, comps[0], comps[1], comps[2])


def equilibrium(rho, momx, momy, momz):
    safe = jnp.maximum(rho, 0.5)
    velx, vely, velz = (momx / safe, momy / safe, momz / safe)
    square = velx * velx + vely * vely + velz * velz
    rows = []
    for index in range(19):
        cx, cy, cz = lattice[index]
        proj = cx * velx + cy * vely + cz * velz
        rows.append(weights[index] * rho * (1.0 + 3.0 * proj + 4.5 * proj * proj - 1.5 * square))
    return jnp.stack(rows, 0)


def collide(f, omega, solid):
    rho, momx, momy, momz = moments(f)
    feq = equilibrium(rho, momx, momy, momz)
    post = f + omega[None] * (feq - f)
    flipped = jnp.stack([f[opposite[index]] for index in range(19)], 0)
    return jnp.where(solid[None], flipped, post)


def stream(padded):
    size_z = padded.shape[1] - 2
    size_x = padded.shape[2] - 2
    size_y = padded.shape[3] - 2
    rows = []
    for index in range(19):
        cx, cy, cz = lattice[index]
        rows.append(
            padded[
                index, 1 - cz : 1 - cz + size_z, 1 - cx : 1 - cx + size_x, 1 - cy : 1 - cy + size_y
            ]
        )
    return jnp.stack(rows, 0)


def per_device(populations, omega, obstacle):
    solid = obstacle == 1
    f = populations
    before = f
    for step in range(STEPS):
        post = collide(f, omega, solid)
        padded = extended(post, (("gx", 2), ("gy", 3), ("gz", 1)), 1)
        f = stream(padded)
        if step == STEPS - 2:
            before = f
    rho_a, jxa, jya, jza = moments(before)
    rho_b, jxb, jyb, jzb = moments(f)
    cells = float(
        f.shape[1]
        * f.shape[2]
        * f.shape[3]
        * lax.axis_size("gx")
        * lax.axis_size("gy")
        * lax.axis_size("gz")
    )
    diff_rho = rho_b - rho_a
    diff_x = jxb - jxa
    diff_y = jyb - jya
    diff_z = jzb - jza
    local_terms = (
        jnp.sum(diff_rho * diff_rho),
        jnp.sum(diff_x * diff_x + diff_y * diff_y + diff_z * diff_z),
        jnp.sum(jxb),
        jnp.sum(jyb),
        jnp.sum(jzb),
        jnp.sum(diff_x),
        jnp.sum(diff_y),
        jnp.sum(diff_z),
        jnp.sum(jxb * jxb + jyb * jyb + jzb * jzb),
        jnp.sum(jxb * diff_x + jyb * diff_y + jzb * diff_z),
    )
    (
        change_rho,
        change_mom,
        base_x,
        base_y,
        base_z,
        delta_x,
        delta_y,
        delta_z,
        energy_base,
        energy_cross,
    ) = lax.psum(
        (
            local_terms[0],
            local_terms[1],
            local_terms[2],
            local_terms[3],
            local_terms[4],
            local_terms[5],
            local_terms[6],
            local_terms[7],
            local_terms[8],
            local_terms[9],
        ),
        ("gx", "gy", "gz"),
    )
    change = (change_rho + change_mom) / cells
    gain = JUMP / (1.0 + limiter * change)
    jxp = jxb + gain * diff_x
    jyp = jyb + gain * diff_y
    jzp = jzb + gain * diff_z
    sum_x = base_x + gain * delta_x
    sum_y = base_y + gain * delta_y
    sum_z = base_z + gain * delta_z
    energy = energy_base + 2.0 * gain * energy_cross + gain * gain * change_mom
    rho_p = rho_b + gain * diff_rho
    lifted = equilibrium(rho_p, jxp, jyp, jzp)
    diagnostics = jnp.stack([change, sum_x / cells, sum_y / cells, sum_z / cells, energy / cells])
    return (lifted, diagnostics)


def solution(mesh):
    in_specs = (P(None, "gz", "gx", "gy"), P("gz", "gx", "gy"), P("gz", "gx", "gy"))
    out_specs = (P(None, "gz", "gx", "gy"), P())
    return jax.shard_map(
        per_device, mesh=mesh, in_specs=in_specs, out_specs=out_specs, check_vma=False
    )
```

profile of v0, /device:TPU:12, one launch (start us, length us, event | category | flops | bytes accessed | tf_op | source)
XLA Modules:
  0.0 191.7 jit_solution(2588128891063399128)
XLA Ops:
  5.9 1.6 collective-permute-start.1
  7.5 2.4 %collective-permute-done = f32[19,8,1,128]{3,2,1,0:T(1,128)S(1)} collective-permute-done((f32[19,8,1,128]{3,2,1,0:T(1,128)S(1)}, f32[19,8,1,128]{3,2,1,0:T(1,128)S(1)}, u32[]{:S(2)}, u32[]{:S(2)}) %collective-permute-start) | collective-permute-done | bytes 77856 | tf_op jit(solution)/shard_map/ppermute | solution.py:42
  9.8 3.4 %collective-permute-done.1 = f32[19,8,1,128]{3,2,1,0:T(1,128)S(1)} collective-permute-done((f32[19,8,1,128]{3,2,1,0:T(1,128)S(1)}, f32[19,8,1,128]{3,2,1,0:T(1,128)S(1)}, u32[]{:S(2)}, u32[]{:S(2)}) %collective-permute-start.1) | collective-permute-done | bytes 77856 | tf_op jit(solution)/shard_map/ppermute | solution.py:41
  16.3 1.4 copy.201
  18.8 1.4 copy.203
  21.2 1.5 collective-permute-start.5
  22.8 8.1 %collective-permute-done.4 = f32[19,1,10,130]{3,2,1,0:T(8,128)S(1)} collective-permute-done((f32[19,1,10,130]{3,2,1,0:T(8,128)S(1)}, f32[19,1,10,130]{3,2,1,0:T(8,128)S(1)}, u32[]{:S(2)}, u32[]{:S(2)}) %collective-permute-start.4) | collective-permute-done | bytes 98832 | tf_op jit(solution)/shard_map/ppermute | solution.py:42
  31.0 6.2 %collective-permute-done.5 = f32[19,1,10,130]{3,2,1,0:T(8,128)S(1)} collective-permute-done((f32[19,1,10,130]{3,2,1,0:T(8,128)S(1)}, f32[19,1,10,130]{3,2,1,0:T(8,128)S(1)}, u32[]{:S(2)}, u32[]{:S(2)}) %collective-permute-start.5) | collective-permute-done | bytes 98832 | tf_op jit(solution)/shard_map/ppermute | solution.py:41
  38.8 2.5 %collective-permute-start.6 = (f32[19,8,1,128]{3,2,1,0:T(1,128)S(1)}, f32[19,8,1,128]{3,2,1,0:T(1,128)S(1)}, u32[]{:S(2)}, u32[]{:S(2)}) collective-permute-start(f32[19,8,1,128]{3,2,1,0:T(1,128)S(1)} %get-tuple-element.150), channel_id=1, source_target_pairs={{8,0},{16,8},{24,16},{0,24},{9,1},{17,9},{25,17},{1,25},{10,2},{18... | collective-permute-start | bytes 233480 | tf_op jit(solution)/shard_map/ppermute | solution.py:42
  41.3 2.0 %collective-permute-done.6 = f32[19,8,1,128]{3,2,1,0:T(1,128)S(1)} collective-permute-done((f32[19,8,1,128]{3,2,1,0:T(1,128)S(1)}, f32[19,8,1,128]{3,2,1,0:T(1,128)S(1)}, u32[]{:S(2)}, u32[]{:S(2)}) %collective-permute-start.6) | collective-permute-done | bytes 77856 | tf_op jit(solution)/shard_map/ppermute | solution.py:42
  43.3 2.4 %collective-permute-done.7 = f32[19,8,1,128]{3,2,1,0:T(1,128)S(1)} collective-permute-done((f32[19,8,1,128]{3,2,1,0:T(1,128)S(1)}, f32[19,8,1,128]{3,2,1,0:T(1,128)S(1)}, u32[]{:S(2)}, u32[]{:S(2)}) %collective-permute-start.7) | collective-permute-done | bytes 77856 | tf_op jit(solution)/shard_map/ppermute | solution.py:41
  51.5 1.4 copy.209
  53.9 1.5 collective-permute-start.11
  55.5 8.1 %collective-permute-done.10 = f32[19,1,10,130]{3,2,1,0:T(8,128)S(1)} collective-permute-done((f32[19,1,10,130]{3,2,1,0:T(8,128)S(1)}, f32[19,1,10,130]{3,2,1,0:T(8,128)S(1)}, u32[]{:S(2)}, u32[]{:S(2)}) %collective-permute-start.10) | collective-permute-done | bytes 98832 | tf_op jit(solution)/shard_map/ppermute | solution.py:42
  63.6 5.0 %collective-permute-done.11 = f32[19,1,10,130]{3,2,1,0:T(8,128)S(1)} collective-permute-done((f32[19,1,10,130]{3,2,1,0:T(8,128)S(1)}, f32[19,1,10,130]{3,2,1,0:T(8,128)S(1)}, u32[]{:S(2)}, u32[]{:S(2)}) %collective-permute-start.11) | collective-permute-done | bytes 98832 | tf_op jit(solution)/shard_map/ppermute | solution.py:41
  70.3 2.4 %collective-permute-start.12 = (f32[19,8,1,128]{3,2,1,0:T(1,128)S(1)}, f32[19,8,1,128]{3,2,1,0:T(1,128)S(1)}, u32[]{:S(2)}, u32[]{:S(2)}) collective-permute-start(f32[19,8,1,128]{3,2,1,0:T(1,128)S(1)} %get-tuple-element.148), channel_id=1, source_target_pairs={{8,0},{16,8},{24,16},{0,24},{9,1},{17,9},{25,17},{1,25},{10,2},{18... | collective-permute-start | bytes 233480 | tf_op jit(solution)/shard_map/ppermute | solution.py:42
  72.6 2.9 %collective-permute-done.12 = f32[19,8,1,128]{3,2,1,0:T(1,128)S(1)} collective-permute-done((f32[19,8,1,128]{3,2,1,0:T(1,128)S(1)}, f32[19,8,1,128]{3,2,1,0:T(1,128)S(1)}, u32[]{:S(2)}, u32[]{:S(2)}) %collective-permute-start.12) | collective-permute-done | bytes 77856 | tf_op jit(solution)/shard_map/ppermute | solution.py:42
  75.6 1.5 collective-permute-done.13
  82.6 1.4 copy.215
  85.1 1.5 collective-permute-start.17
  86.7 8.1 %collective-permute-done.16 = f32[19,1,10,130]{3,2,1,0:T(8,128)S(1)} collective-permute-done((f32[19,1,10,130]{3,2,1,0:T(8,128)S(1)}, f32[19,1,10,130]{3,2,1,0:T(8,128)S(1)}, u32[]{:S(2)}, u32[]{:S(2)}) %collective-permute-start.16) | collective-permute-done | bytes 98832 | tf_op jit(solution)/shard_map/ppermute | solution.py:42
  94.8 6.2 %collective-permute-done.17 = f32[19,1,10,130]{3,2,1,0:T(8,128)S(1)} collective-permute-done((f32[19,1,10,130]{3,2,1,0:T(8,128)S(1)}, f32[19,1,10,130]{3,2,1,0:T(8,128)S(1)}, u32[]{:S(2)}, u32[]{:S(2)}) %collective-permute-start.17) | collective-permute-done | bytes 98832 | tf_op jit(solution)/shard_map/ppermute | solution.py:41
  104.3 1.6 collective-permute-start.19
  105.9 2.3 %collective-permute-done.18 = f32[19,8,1,128]{3,2,1,0:T(1,128)S(1)} collective-permute-done((f32[19,8,1,128]{3,2,1,0:T(1,128)S(1)}, f32[19,8,1,128]{3,2,1,0:T(1,128)S(1)}, u32[]{:S(2)}, u32[]{:S(2)}) %collective-permute-start.18) | collective-permute-done | bytes 77856 | tf_op jit(solution)/shard_map/ppermute | solution.py:41
  112.2 1.8 collective-permute-start.21
  115.2 1.4 copy.219
  116.6 2.2 %copy.221 = f32[19,8,10,1]{3,2,1,0:T(8,128)S(1)} copy(f32[19,8,10,1]{0,1,3,2:T(8,128)} %collective-permute-done.21) | data formatting | bytes 12160 | tf_op jit(solution)/shard_map/ppermute | solution.py:42
  119.9 1.6 collective-permute-start.23
  121.5 8.1 %collective-permute-done.22 = f32[19,1,10,130]{3,2,1,0:T(8,128)S(1)} collective-permute-done((f32[19,1,10,130]{3,2,1,0:T(8,128)S(1)}, f32[19,1,10,130]{3,2,1,0:T(8,128)S(1)}, u32[]{:S(2)}, u32[]{:S(2)}) %collective-permute-start.22) | collective-permute-done | bytes 98832 | tf_op jit(solution)/shard_map/ppermute | solution.py:41
  129.6 4.6 %collective-permute-done.23 = f32[19,1,10,130]{3,2,1,0:T(8,128)S(1)} collective-permute-done((f32[19,1,10,130]{3,2,1,0:T(8,128)S(1)}, f32[19,1,10,130]{3,2,1,0:T(8,128)S(1)}, u32[]{:S(2)}, u32[]{:S(2)}) %collective-permute-start.23) | collective-permute-done | bytes 98832 | tf_op jit(solution)/shard_map/ppermute | solution.py:42
  136.4 1.5 fusion.287
  137.9 44.2 %all-reduce = (f32[]{:T(128)}, f32[]{:T(128)}, f32[]{:T(128)}, f32[]{:T(128)}, f32[]{:T(128)}, /*index=5*/f32[]{:T(128)}, f32[]{:T(128)}, f32[]{:T(128)}, f32[]{:T(128)}, f32[]{:T(128)}) all-reduce(f32[]{:T(128)} %fusion.287, f32[]{:T(128)} %get-tuple-element.5, ...), channel_id=1, replica_groups=mesh['gx'=4,'gy'=4,'gz'=2] {'gx','gy','gz'}, use_global_device_ids=true, to_apply=%region_2.3 | all-reduce | flops 10 | bytes 80 | tf_op jit(solution)/shard_map/psum | solution.py:142
  (373 shorter events, 39.5 us)
Async XLA Ops:
  5.4 4.5 %collective-permute-start = (f32[19,8,1,128]{3,2,1,0:T(1,128)S(1)}, f32[19,8,1,128]{3,2,1,0:T(1,128)S(1)}, u32[]{:S(2)}, u32[]{:S(2)}) collective-permute-start(f32[19,8,1,128]{3,2,1,0:T(1,128)S(1)} %get-tuple-element.152), channel_id=1, source_target_pairs={{8,0},{16,8},{24,16},{0,24},{9,1},{17,9},{25,17},{1,25},{10,2},{18... | collective-permute-start | bytes 233480 | tf_op jit(solution)/shard_map/ppermute | solution.py:42
  5.9 7.3 %collective-permute-start.1 = (f32[19,8,1,128]{3,2,1,0:T(1,128)S(1)}, f32[19,8,1,128]{3,2,1,0:T(1,128)S(1)}, u32[]{:S(2)}, u32[]{:S(2)}) collective-permute-start(f32[19,8,1,128]{3,2,1,0:T(1,128)S(1)} %get-tuple-element.151), channel_id=1, source_target_pairs={{0,8},{8,16},{16,24},{24,0},{1,9},{9,17},{17,25},{25,1},{2,10},{10... | collective-permute-start | bytes 233480 | tf_op jit(solution)/shard_map/ppermute | solution.py:41
  14.6 1.7 collective-permute-start.2
  15.4 3.5 %collective-permute-start.3 = (f32[19,8,10,1]{0,1,3,2:T(8,128)S(1)}, f32[19,8,10,1]{0,1,3,2:T(8,128)S(1)}, u32[]{:S(2)}, u32[]{:S(2)}) collective-permute-start(f32[19,8,10,1]{0,1,3,2:T(8,128)S(1)} %copy.202), channel_id=1, source_target_pairs={{0,2},{2,4},{4,6},{6,0},{1,3},{3,5},{5,7},{7,1},{8,10},{10,12},{12... | collective-permute-start | bytes 18248 | tf_op jit(solution)/shard_map/ppermute | solution.py:41
  20.7 10.3 %collective-permute-start.4 = (f32[19,1,10,130]{3,2,1,0:T(8,128)S(1)}, f32[19,1,10,130]{3,2,1,0:T(8,128)S(1)}, u32[]{:S(2)}, u32[]{:S(2)}) collective-permute-start(f32[19,1,10,130]{3,2,1,0:T(8,128)S(1)} %get-tuple-element.136), channel_id=1, source_target_pairs={{1,0},{0,1},{3,2},{2,3},{5,4},{4,5},{7,6},{6,7},{9,8},{8,9},{11,10... | collective-permute-start | bytes 296408 | tf_op jit(solution)/shard_map/ppermute | solution.py:42
  21.2 15.9 %collective-permute-start.5 = (f32[19,1,10,130]{3,2,1,0:T(8,128)S(1)}, f32[19,1,10,130]{3,2,1,0:T(8,128)S(1)}, u32[]{:S(2)}, u32[]{:S(2)}) collective-permute-start(f32[19,1,10,130]{3,2,1,0:T(8,128)S(1)} %get-tuple-element.135), channel_id=1, source_target_pairs={{0,1},{1,0},{2,3},{3,2},{4,5},{5,4},{6,7},{7,6},{8,9},{9,8},{10,11... | collective-permute-start | bytes 296408 | tf_op jit(solution)/shard_map/ppermute | solution.py:41
  38.8 4.5 %collective-permute-start.6 = (f32[19,8,1,128]{3,2,1,0:T(1,128)S(1)}, f32[19,8,1,128]{3,2,1,0:T(1,128)S(1)}, u32[]{:S(2)}, u32[]{:S(2)}) collective-permute-start(f32[19,8,1,128]{3,2,1,0:T(1,128)S(1)} %get-tuple-element.150), channel_id=1, source_target_pairs={{8,0},{16,8},{24,16},{0,24},{9,1},{17,9},{25,17},{1,25},{10,2},{18... | collective-permute-start | bytes 233480 | tf_op jit(solution)/shard_map/ppermute | solution.py:42
  41.3 4.5 %collective-permute-start.7 = (f32[19,8,1,128]{3,2,1,0:T(1,128)S(1)}, f32[19,8,1,128]{3,2,1,0:T(1,128)S(1)}, u32[]{:S(2)}, u32[]{:S(2)}) collective-permute-start(f32[19,8,1,128]{3,2,1,0:T(1,128)S(1)} %get-tuple-element.149), channel_id=1, source_target_pairs={{0,8},{8,16},{16,24},{24,0},{1,9},{9,17},{17,25},{25,1},{2,10},{10... | collective-permute-start | bytes 233480 | tf_op jit(solution)/shard_map/ppermute | solution.py:41
  47.1 1.7 collective-permute-start.8
  47.9 3.6 %collective-permute-start.9 = (f32[19,8,10,1]{0,1,3,2:T(8,128)S(1)}, f32[19,8,10,1]{0,1,3,2:T(8,128)S(1)}, u32[]{:S(2)}, u32[]{:S(2)}) collective-permute-start(f32[19,8,10,1]{0,1,3,2:T(8,128)S(1)} %copy.208), channel_id=1, source_target_pairs={{0,2},{2,4},{4,6},{6,0},{1,3},{3,5},{5,7},{7,1},{8,10},{10,12},{12... | collective-permute-start | bytes 18248 | tf_op jit(solution)/shard_map/ppermute | solution.py:41
  53.3 10.3 %collective-permute-start.10 = (f32[19,1,10,130]{3,2,1,0:T(8,128)S(1)}, f32[19,1,10,130]{3,2,1,0:T(8,128)S(1)}, u32[]{:S(2)}, u32[]{:S(2)}) collective-permute-start(f32[19,1,10,130]{3,2,1,0:T(8,128)S(1)} %get-tuple-element.134), channel_id=1, source_target_pairs={{1,0},{0,1},{3,2},{2,3},{5,4},{4,5},{7,6},{6,7},{9,8},{8,9},{11,10... | collective-permute-start | bytes 296408 | tf_op jit(solution)/shard_map/ppermute | solution.py:42
  53.9 14.8 %collective-permute-start.11 = (f32[19,1,10,130]{3,2,1,0:T(8,128)S(1)}, f32[19,1,10,130]{3,2,1,0:T(8,128)S(1)}, u32[]{:S(2)}, u32[]{:S(2)}) collective-permute-start(f32[19,1,10,130]{3,2,1,0:T(8,128)S(1)} %get-tuple-element.133), channel_id=1, source_target_pairs={{0,1},{1,0},{2,3},{3,2},{4,5},{5,4},{6,7},{7,6},{8,9},{9,8},{10,11... | collective-permute-start | bytes 296408 | tf_op jit(solution)/shard_map/ppermute | solution.py:41
  70.2 30.9 %copy-start = (f32[19,8,8,128]{3,2,1,0:T(8,128)}, f32[19,8,8,128]{3,2,1,0:T(8,128)S(1)}, u32[]{:S(2)}) copy-start(f32[19,8,8,128]{3,2,1,0:T(8,128)S(1)} %add_select_fusion.1) | copy-start | bytes 1867780
  70.3 5.3 %collective-permute-start.12 = (f32[19,8,1,128]{3,2,1,0:T(1,128)S(1)}, f32[19,8,1,128]{3,2,1,0:T(1,128)S(1)}, u32[]{:S(2)}, u32[]{:S(2)}) collective-permute-start(f32[19,8,1,128]{3,2,1,0:T(1,128)S(1)} %get-tuple-element.148), channel_id=1, source_target_pairs={{8,0},{16,8},{24,16},{0,24},{9,1},{17,9},{25,17},{1,25},{10,2},{18... | collective-permute-start | bytes 233480 | tf_op jit(solution)/shard_map/ppermute | solution.py:42
  72.6 4.4 %collective-permute-start.13 = (f32[19,8,1,128]{3,2,1,0:T(1,128)S(1)}, f32[19,8,1,128]{3,2,1,0:T(1,128)S(1)}, u32[]{:S(2)}, u32[]{:S(2)}) collective-permute-start(f32[19,8,1,128]{3,2,1,0:T(1,128)S(1)} %get-tuple-element.147), channel_id=1, source_target_pairs={{0,8},{8,16},{16,24},{24,0},{1,9},{9,17},{17,25},{25,1},{2,10},{10... | collective-permute-start | bytes 233480 | tf_op jit(solution)/shard_map/ppermute | solution.py:41
  78.4 1.7 collective-permute-start.14
  79.2 3.5 %collective-permute-start.15 = (f32[19,8,10,1]{0,1,3,2:T(8,128)S(1)}, f32[19,8,10,1]{0,1,3,2:T(8,128)S(1)}, u32[]{:S(2)}, u32[]{:S(2)}) collective-permute-start(f32[19,8,10,1]{0,1,3,2:T(8,128)S(1)} %copy.214), channel_id=1, source_target_pairs={{0,2},{2,4},{4,6},{6,0},{1,3},{3,5},{5,7},{7,1},{8,10},{10,12},{12... | collective-permute-start | bytes 18248 | tf_op jit(solution)/shard_map/ppermute | solution.py:41
  84.5 16.5 %copy-start.25 = (f32[19,8,1,128]{3,2,1,0:T(1,128)S(1)}, f32[19,8,1,128]{3,2,1,0:T(1,128)}, u32[]{:S(2)}) copy-start(f32[19,8,1,128]{3,2,1,0:T(1,128)} %copy-done.24) | copy-start | bytes 233476
  84.5 16.5 %copy-start.27 = (f32[19,8,1,128]{3,2,1,0:T(1,128)S(1)}, f32[19,8,1,128]{3,2,1,0:T(1,128)}, u32[]{:S(2)}) copy-start(f32[19,8,1,128]{3,2,1,0:T(1,128)} %copy-done.26) | copy-start | bytes 233476
  84.5 10.3 %collective-permute-start.16 = (f32[19,1,10,130]{3,2,1,0:T(8,128)S(1)}, f32[19,1,10,130]{3,2,1,0:T(8,128)S(1)}, u32[]{:S(2)}, u32[]{:S(2)}) collective-permute-start(f32[19,1,10,130]{3,2,1,0:T(8,128)S(1)} %get-tuple-element.132), channel_id=1, source_target_pairs={{1,0},{0,1},{3,2},{2,3},{5,4},{4,5},{7,6},{6,7},{9,8},{8,9},{11,10... | collective-permute-start | bytes 296408 | tf_op jit(solution)/shard_map/ppermute | solution.py:42
  85.1 15.9 %collective-permute-start.17 = (f32[19,1,10,130]{3,2,1,0:T(8,128)S(1)}, f32[19,1,10,130]{3,2,1,0:T(8,128)S(1)}, u32[]{:S(2)}, u32[]{:S(2)}) collective-permute-start(f32[19,1,10,130]{3,2,1,0:T(8,128)S(1)} %get-tuple-element.131), channel_id=1, source_target_pairs={{0,1},{1,0},{2,3},{3,2},{4,5},{5,4},{6,7},{7,6},{8,9},{9,8},{10,11... | collective-permute-start | bytes 296408 | tf_op jit(solution)/shard_map/ppermute | solution.py:41
  103.3 5.0 %collective-permute-start.18 = (f32[19,8,1,128]{3,2,1,0:T(1,128)S(1)}, f32[19,8,1,128]{3,2,1,0:T(1,128)S(1)}, u32[]{:S(2)}, u32[]{:S(2)}) collective-permute-start(f32[19,8,1,128]{3,2,1,0:T(1,128)S(1)} %get-tuple-element.146), channel_id=1, source_target_pairs={{0,8},{8,16},{16,24},{24,0},{1,9},{9,17},{17,25},{25,1},{2,10},{10... | collective-permute-start | bytes 233480 | tf_op jit(solution)/shard_map/ppermute | solution.py:41
  104.3 5.2 %collective-permute-start.19 = (f32[19,8,1,128]{3,2,1,0:T(1,128)S(1)}, f32[19,8,1,128]{3,2,1,0:T(1,128)S(1)}, u32[]{:S(2)}, u32[]{:S(2)}) collective-permute-start(f32[19,8,1,128]{3,2,1,0:T(1,128)S(1)} %get-tuple-element.145), channel_id=1, source_target_pairs={{8,0},{16,8},{24,16},{0,24},{9,1},{17,9},{25,17},{1,25},{10,2},{18... | collective-permute-start | bytes 233480 | tf_op jit(solution)/shard_map/ppermute | solution.py:42
  111.5 3.7 %collective-permute-start.20 = (f32[19,8,10,1]{0,1,3,2:T(8,128)}, f32[19,8,10,1]{0,1,3,2:T(8,128)S(1)}, u32[]{:S(2)}, u32[]{:S(2)}) collective-permute-start(f32[19,8,10,1]{0,1,3,2:T(8,128)} %copy.218), channel_id=1, source_target_pairs={{0,2},{2,4},{4,6},{6,0},{1,3},{3,5},{5,7},{7,1},{8,10},{10,12},{12... | collective-permute-start | bytes 18248 | tf_op jit(solution)/shard_map/ppermute | solution.py:41
  112.2 4.4 %collective-permute-start.21 = (f32[19,8,10,1]{0,1,3,2:T(8,128)S(1)}, f32[19,8,10,1]{0,1,3,2:T(8,128)}, u32[]{:S(2)}, u32[]{:S(2)}) collective-permute-start(f32[19,8,10,1]{0,1,3,2:T(8,128)S(1)} %copy.220), channel_id=1, source_target_pairs={{2,0},{4,2},{6,4},{0,6},{3,1},{5,3},{7,5},{1,7},{10,8},{12,10},{14... | collective-permute-start | bytes 18248 | tf_op jit(solution)/shard_map/ppermute | solution.py:42
  118.8 15.5 %copy-start.7 = (f32[1,8,8,128]{3,2,1,0:T(8,128)S(1)}, f32[1,8,8,128]{3,2,1,0:T(8,128)}, u32[]{:S(2)}) copy-start(f32[1,8,8,128]{3,2,1,0:T(8,128)} %copy-done.6) | copy-start | bytes 98308
  118.8 15.5 %copy-start.9 = (f32[1,8,8,128]{3,2,1,0:T(8,128)S(1)}, f32[1,8,8,128]{3,2,1,0:T(8,128)}, u32[]{:S(2)}) copy-start(f32[1,8,8,128]{3,2,1,0:T(8,128)} %copy-done.8) | copy-start | bytes 98308
  118.8 15.4 %copy-start.11 = (f32[1,8,8,128]{3,2,1,0:T(8,128)S(1)}, f32[1,8,8,128]{3,2,1,0:T(8,128)}, u32[]{:S(2)}) copy-start(f32[1,8,8,128]{3,2,1,0:T(8,128)} %copy-done.10) | copy-start | bytes 98308
  118.8 15.4 %copy-start.15 = (f32[1,8,8,128]{3,2,1,0:T(8,128)S(1)}, f32[1,8,8,128]{3,2,1,0:T(8,128)}, u32[]{:S(2)}) copy-start(f32[1,8,8,128]{3,2,1,0:T(8,128)} %copy-done.14) | copy-start | bytes 98308
  118.8 15.4 %copy-start.21 = (f32[1,8,8,128]{3,2,1,0:T(8,128)S(1)}, f32[1,8,8,128]{3,2,1,0:T(8,128)}, u32[]{:S(2)}) copy-start(f32[1,8,8,128]{3,2,1,0:T(8,128)} %copy-done.20) | copy-start | bytes 98308
  119.3 10.3 %collective-permute-start.22 = (f32[19,1,10,130]{3,2,1,0:T(8,128)S(1)}, f32[19,1,10,130]{3,2,1,0:T(8,128)S(1)}, u32[]{:S(2)}, u32[]{:S(2)}) collective-permute-start(f32[19,1,10,130]{3,2,1,0:T(8,128)S(1)} %get-tuple-element.129), channel_id=1, source_target_pairs={{0,1},{1,0},{2,3},{3,2},{4,5},{5,4},{6,7},{7,6},{8,9},{9,8},{10,11... | collective-permute-start | bytes 296408 | tf_op jit(solution)/shard_map/ppermute | solution.py:41
  119.9 14.3 %collective-permute-start.23 = (f32[19,1,10,130]{3,2,1,0:T(8,128)S(1)}, f32[19,1,10,130]{3,2,1,0:T(8,128)S(1)}, u32[]{:S(2)}, u32[]{:S(2)}) collective-permute-start(f32[19,1,10,130]{3,2,1,0:T(8,128)S(1)} %get-tuple-element.130), channel_id=1, source_target_pairs={{1,0},{0,1},{3,2},{2,3},{5,4},{4,5},{7,6},{6,7},{9,8},{8,9},{11,10... | collective-permute-start | bytes 296408 | tf_op jit(solution)/shard_map/ppermute | solution.py:42
  (48 other events, 172.3 us)
where the time goes:
time: 193 us; the launch traced here: 192 us
  waiting for transfers between devices  78.8 us (41%)
  blocking collectives  44.2 us (23%)
  local copies, waits for them, and re-layouts  23.9 us (12%)
  starting transfers between devices  21.7 us (11%)
  other arithmetic  13.1 us (7%)
  between operations  9.94 us (5%)
    psum x1, blocking collectives, per_device(): lax.psum((local_terms[0], local_terms[1], local_terms[2], local_terms[3],...  44.2 us
    ppermute x12, waiting for transfers between devices, extended(): before = lax.ppermute(last, axis, up)  39.9 us
    ppermute x12, waiting for transfers between devices, extended(): after = lax.ppermute(first, axis, down)  38.8 us
    ppermute x12, starting transfers between devices, extended(): after = lax.ppermute(first, axis, down)  12.2 us
    ppermute x12, starting transfers between devices, extended(): before = lax.ppermute(last, axis, up)  9.54 us
    ppermute x4, local copies, waits for them, and re-layouts, extended(): after = lax.ppermute(first, axis, down)  6.25 us
    unnamed x90, other arithmetic  5.58 us
    ppermute x4, local copies, waits for them, and re-layouts, extended(): before = lax.ppermute(last, axis, up)  5.46 us
  transfers between devices with their start and end apart: 24, of which 23 were waited for; matrix products, arithmetic and copies ran while one was open for 4% of the time, Pallas kernels for 0%

commit v1 on v0

--- a/solution.py
+++ b/solution.py
@@ -29,6 +29,11 @@
 weights = [1.0 / 3.0] + [1.0 / 18.0] * 6 + [1.0 / 36.0] * 12
 opposite = [0, 2, 1, 4, 3, 6, 5, 8, 7, 10, 9, 12, 11, 14, 13, 16, 15, 18, 17]
 limiter = 25.0
+
+
+def axis_by_axis(array, inner_axis, outer_axis):
+    half = lax.psum(array, inner_axis)
+    return lax.psum(half, outer_axis)
 
 
 def extended(x, sides, width):
@@ -139,7 +144,7 @@
         delta_z,
         energy_base,
         energy_cross,
-    ) = lax.psum(
+    ) = axis_by_axis(
         (
             local_terms[0],
             local_terms[1],
@@ -152,7 +157,8 @@
             local_terms[8],
             local_terms[9],
         ),
-        ("gx", "gy", "gz"),
+        ("gy", "gz"),
+        "gx",
     )
     change = (change_rho + change_mom) / cells
     gain = JUMP / (1.0 + limiter * change)

time: 193 us -> 180 us (0.933)
  the two profiles are of different devices: /device:TPU:12 before, /device:TPU:0 now
where the time goes in v1:
time: 180 us; the launch traced here: 179 us
  waiting for transfers between devices  79.2 us (44%)
  blocking collectives  27.8 us (15%)
  starting transfers between devices  25.2 us (14%)
  local copies, waits for them, and re-layouts  23.9 us (13%)
  other arithmetic  13.1 us (7%)
  between operations  9.92 us (6%)
    ppermute x12, waiting for transfers between devices, extended(): before = lax.ppermute(last, axis, up)  41.7 us
    ppermute x12, waiting for transfers between devices, extended(): after = lax.ppermute(first, axis, down)  37.6 us
    ppermute x12, starting transfers between devices, extended(): after = lax.ppermute(first, axis, down)  16.9 us
    psum x1, blocking collectives, axis_by_axis(): half = lax.psum(array, inner_axis)  14.7 us
    psum x1, blocking collectives, axis_by_axis(): return lax.psum(half, outer_axis)  13.1 us
    ppermute x12, starting transfers between devices, extended(): before = lax.ppermute(last, axis, up)  8.35 us
    ppermute x4, local copies, waits for them, and re-layouts, extended(): after = lax.ppermute(first, axis, down)  6.25 us
    unnamed x90, other arithmetic  5.58 us
  transfers between devices with their start and end apart: 24, of which 22 were waited for; matrix products, arithmetic and copies ran while one was open for 5% of the time, Pallas kernels for 0%

profile of v1, /device:TPU:0, one launch (start us, length us, event | category | flops | bytes accessed | tf_op | source)
XLA Modules:
  0.0 179.2 jit_solution(12202767819091923919)
XLA Ops:
  5.4 5.1 %collective-permute-start = (f32[19,8,1,128]{3,2,1,0:T(1,128)S(1)}, f32[19,8,1,128]{3,2,1,0:T(1,128)S(1)}, u32[]{:S(2)}, u32[]{:S(2)}) collective-permute-start(f32[19,8,1,128]{3,2,1,0:T(1,128)S(1)} %get-tuple-element.162), channel_id=1, source_target_pairs={{8,0},{16,8},{24,16},{0,24},{9,1},{17,9},{25,17},{1,25},{10,2},{18... | collective-permute-start | bytes 233480 | tf_op jit(solution)/shard_map/ppermute | solution.py:47
  10.5 2.4 %collective-permute-done = f32[19,8,1,128]{3,2,1,0:T(1,128)S(1)} collective-permute-done((f32[19,8,1,128]{3,2,1,0:T(1,128)S(1)}, f32[19,8,1,128]{3,2,1,0:T(1,128)S(1)}, u32[]{:S(2)}, u32[]{:S(2)}) %collective-permute-start) | collective-permute-done | bytes 77856 | tf_op jit(solution)/shard_map/ppermute | solution.py:47
  13.0 3.7 %collective-permute-done.1 = f32[19,8,1,128]{3,2,1,0:T(1,128)S(1)} collective-permute-done((f32[19,8,1,128]{3,2,1,0:T(1,128)S(1)}, f32[19,8,1,128]{3,2,1,0:T(1,128)S(1)}, u32[]{:S(2)}, u32[]{:S(2)}) %collective-permute-start.1) | collective-permute-done | bytes 77856 | tf_op jit(solution)/shard_map/ppermute | solution.py:46
  22.3 1.4 copy.203
  24.1 1.6 collective-permute-start.4
  26.3 8.1 %collective-permute-done.4 = f32[19,1,10,130]{3,2,1,0:T(8,128)S(1)} collective-permute-done((f32[19,1,10,130]{3,2,1,0:T(8,128)S(1)}, f32[19,1,10,130]{3,2,1,0:T(8,128)S(1)}, u32[]{:S(2)}, u32[]{:S(2)}) %collective-permute-start.4) | collective-permute-done | bytes 98832 | tf_op jit(solution)/shard_map/ppermute | solution.py:47
  34.4 6.2 %collective-permute-done.5 = f32[19,1,10,130]{3,2,1,0:T(8,128)S(1)} collective-permute-done((f32[19,1,10,130]{3,2,1,0:T(8,128)S(1)}, f32[19,1,10,130]{3,2,1,0:T(8,128)S(1)}, u32[]{:S(2)}, u32[]{:S(2)}) %collective-permute-start.5) | collective-permute-done | bytes 98832 | tf_op jit(solution)/shard_map/ppermute | solution.py:46
  42.8 1.5 collective-permute-start.7
  44.3 2.4 %collective-permute-done.6 = f32[19,8,1,128]{3,2,1,0:T(1,128)S(1)} collective-permute-done((f32[19,8,1,128]{3,2,1,0:T(1,128)S(1)}, f32[19,8,1,128]{3,2,1,0:T(1,128)S(1)}, u32[]{:S(2)}, u32[]{:S(2)}) %collective-permute-start.6) | collective-permute-done | bytes 77856 | tf_op jit(solution)/shard_map/ppermute | solution.py:47
  46.7 2.3 %collective-permute-done.7 = f32[19,8,1,128]{3,2,1,0:T(1,128)S(1)} collective-permute-done((f32[19,8,1,128]{3,2,1,0:T(1,128)S(1)}, f32[19,8,1,128]{3,2,1,0:T(1,128)S(1)}, u32[]{:S(2)}, u32[]{:S(2)}) %collective-permute-start.7) | collective-permute-done | bytes 77856 | tf_op jit(solution)/shard_map/ppermute | solution.py:46
  54.8 1.4 copy.209
  56.6 1.6 collective-permute-start.10
  58.8 8.1 %collective-permute-done.10 = f32[19,1,10,130]{3,2,1,0:T(8,128)S(1)} collective-permute-done((f32[19,1,10,130]{3,2,1,0:T(8,128)S(1)}, f32[19,1,10,130]{3,2,1,0:T(8,128)S(1)}, u32[]{:S(2)}, u32[]{:S(2)}) %collective-permute-start.10) | collective-permute-done | bytes 98832 | tf_op jit(solution)/shard_map/ppermute | solution.py:47
  66.9 5.1 %collective-permute-done.11 = f32[19,1,10,130]{3,2,1,0:T(8,128)S(1)} collective-permute-done((f32[19,1,10,130]{3,2,1,0:T(8,128)S(1)}, f32[19,1,10,130]{3,2,1,0:T(8,128)S(1)}, u32[]{:S(2)}, u32[]{:S(2)}) %collective-permute-start.11) | collective-permute-done | bytes 98832 | tf_op jit(solution)/shard_map/ppermute | solution.py:46
  73.8 1.9 %collective-permute-start.13 = (f32[19,8,1,128]{3,2,1,0:T(1,128)S(1)}, f32[19,8,1,128]{3,2,1,0:T(1,128)S(1)}, u32[]{:S(2)}, u32[]{:S(2)}) collective-permute-start(f32[19,8,1,128]{3,2,1,0:T(1,128)S(1)} %get-tuple-element.157), channel_id=1, source_target_pairs={{0,8},{8,16},{16,24},{24,0},{1,9},{9,17},{17,25},{25,1},{2,10},{10... | collective-permute-start | bytes 233480 | tf_op jit(solution)/shard_map/ppermute | solution.py:46
  75.7 2.7 %collective-permute-done.12 = f32[19,8,1,128]{3,2,1,0:T(1,128)S(1)} collective-permute-done((f32[19,8,1,128]{3,2,1,0:T(1,128)S(1)}, f32[19,8,1,128]{3,2,1,0:T(1,128)S(1)}, u32[]{:S(2)}, u32[]{:S(2)}) %collective-permute-start.12) | collective-permute-done | bytes 77856 | tf_op jit(solution)/shard_map/ppermute | solution.py:47
  78.4 1.5 collective-permute-done.13
  84.4 1.6 collective-permute-done.15
  87.9 1.6 collective-permute-start.16
  90.1 8.1 %collective-permute-done.16 = f32[19,1,10,130]{3,2,1,0:T(8,128)S(1)} collective-permute-done((f32[19,1,10,130]{3,2,1,0:T(8,128)S(1)}, f32[19,1,10,130]{3,2,1,0:T(8,128)S(1)}, u32[]{:S(2)}, u32[]{:S(2)}) %collective-permute-start.16) | collective-permute-done | bytes 98832 | tf_op jit(solution)/shard_map/ppermute | solution.py:47
  98.2 6.4 %collective-permute-done.17 = f32[19,1,10,130]{3,2,1,0:T(8,128)S(1)} collective-permute-done((f32[19,1,10,130]{3,2,1,0:T(8,128)S(1)}, f32[19,1,10,130]{3,2,1,0:T(8,128)S(1)}, u32[]{:S(2)}, u32[]{:S(2)}) %collective-permute-start.17) | collective-permute-done | bytes 98832 | tf_op jit(solution)/shard_map/ppermute | solution.py:46
  106.9 3.8 %collective-permute-start.19 = (f32[19,8,1,128]{3,2,1,0:T(1,128)S(1)}, f32[19,8,1,128]{3,2,1,0:T(1,128)S(1)}, u32[]{:S(2)}, u32[]{:S(2)}) collective-permute-start(f32[19,8,1,128]{3,2,1,0:T(1,128)S(1)} %get-tuple-element.155), channel_id=1, source_target_pairs={{8,0},{16,8},{24,16},{0,24},{9,1},{17,9},{25,17},{1,25},{10,2},{18... | collective-permute-start | bytes 233480 | tf_op jit(solution)/shard_map/ppermute | solution.py:47
  110.7 2.9 %collective-permute-done.18 = f32[19,8,1,128]{3,2,1,0:T(1,128)S(1)} collective-permute-done((f32[19,8,1,128]{3,2,1,0:T(1,128)S(1)}, f32[19,8,1,128]{3,2,1,0:T(1,128)S(1)}, u32[]{:S(2)}, u32[]{:S(2)}) %collective-permute-start.18) | collective-permute-done | bytes 77856 | tf_op jit(solution)/shard_map/ppermute | solution.py:46
  116.3 1.8 collective-permute-start.21
  118.0 1.4 collective-permute-done.20
  120.8 2.2 %copy.221 = f32[19,8,10,1]{3,2,1,0:T(8,128)S(1)} copy(f32[19,8,10,1]{0,1,3,2:T(8,128)} %collective-permute-done.21) | data formatting | bytes 12160 | tf_op jit(solution)/shard_map/ppermute | solution.py:47
  123.5 1.6 collective-permute-start.22
  125.7 8.1 %collective-permute-done.22 = f32[19,1,10,130]{3,2,1,0:T(8,128)S(1)} collective-permute-done((f32[19,1,10,130]{3,2,1,0:T(8,128)S(1)}, f32[19,1,10,130]{3,2,1,0:T(8,128)S(1)}, u32[]{:S(2)}, u32[]{:S(2)}) %collective-permute-start.22) | collective-permute-done | bytes 98832 | tf_op jit(solution)/shard_map/ppermute | solution.py:46
  133.8 4.5 %collective-permute-done.23 = f32[19,1,10,130]{3,2,1,0:T(8,128)S(1)} collective-permute-done((f32[19,1,10,130]{3,2,1,0:T(8,128)S(1)}, f32[19,1,10,130]{3,2,1,0:T(8,128)S(1)}, u32[]{:S(2)}, u32[]{:S(2)}) %collective-permute-start.23) | collective-permute-done | bytes 98832 | tf_op jit(solution)/shard_map/ppermute | solution.py:47
  140.4 1.5 fusion.287
  141.9 14.7 %all-reduce = (f32[]{:T(128)}, f32[]{:T(128)}, f32[]{:T(128)}, f32[]{:T(128)}, f32[]{:T(128)}, /*index=5*/f32[]{:T(128)}, f32[]{:T(128)}, f32[]{:T(128)}, f32[]{:T(128)}, f32[]{:T(128)}) all-reduce(f32[]{:T(128)} %fusion.287, f32[]{:T(128)} %get-tuple-element.5, ...), channel_id=1, replica_groups=mesh['gx'=4,'gy'=4,'gz'=2] {'gy','gz'}, use_global_device_ids=true, to_apply=%region_2.3 | all-reduce | flops 10 | bytes 80 | tf_op jit(solution)/shard_map/psum | solution.py:35
  156.7 13.1 %all-reduce.1 = (f32[]{:T(128)}, f32[]{:T(128)}, f32[]{:T(128)}, f32[]{:T(128)}, f32[]{:T(128)}, /*index=5*/f32[]{:T(128)}, f32[]{:T(128)}, f32[]{:T(128)}, f32[]{:T(128)}, f32[]{:T(128)}) all-reduce(f32[]{:T(128)} %get-tuple-element.13, f32[]{:T(128)} %get-tuple-element.14, ...), channel_id=1, replica_groups=mesh['gx'=4,'gy'=4,'gz'=2] {'gx'}, use_global_device_ids=true, to_apply=%region_3.4 | all-reduce | flops 10 | bytes 80 | tf_op jit(solution)/shard_map/psum | solution.py:36
  (374 shorter events, 39.0 us)
Async XLA Ops:
  5.4 7.6 %collective-permute-start = (f32[19,8,1,128]{3,2,1,0:T(1,128)S(1)}, f32[19,8,1,128]{3,2,1,0:T(1,128)S(1)}, u32[]{:S(2)}, u32[]{:S(2)}) collective-permute-start(f32[19,8,1,128]{3,2,1,0:T(1,128)S(1)} %get-tuple-element.162), channel_id=1, source_target_pairs={{8,0},{16,8},{24,16},{0,24},{9,1},{17,9},{25,17},{1,25},{10,2},{18... | collective-permute-start | bytes 233480 | tf_op jit(solution)/shard_map/ppermute | solution.py:47
  10.5 6.2 %collective-permute-start.1 = (f32[19,8,1,128]{3,2,1,0:T(1,128)S(1)}, f32[19,8,1,128]{3,2,1,0:T(1,128)S(1)}, u32[]{:S(2)}, u32[]{:S(2)}) collective-permute-start(f32[19,8,1,128]{3,2,1,0:T(1,128)S(1)} %get-tuple-element.161), channel_id=1, source_target_pairs={{0,8},{8,16},{16,24},{24,0},{1,9},{9,17},{17,25},{25,1},{2,10},{10... | collective-permute-start | bytes 233480 | tf_op jit(solution)/shard_map/ppermute | solution.py:46
  18.1 1.7 collective-permute-start.2
  18.8 3.5 %collective-permute-start.3 = (f32[19,8,10,1]{0,1,3,2:T(8,128)S(1)}, f32[19,8,10,1]{0,1,3,2:T(8,128)S(1)}, u32[]{:S(2)}, u32[]{:S(2)}) collective-permute-start(f32[19,8,10,1]{0,1,3,2:T(8,128)S(1)} %copy.202), channel_id=1, source_target_pairs={{0,2},{2,4},{4,6},{6,0},{1,3},{3,5},{5,7},{7,1},{8,10},{10,12},{12... | collective-permute-start | bytes 18248 | tf_op jit(solution)/shard_map/ppermute | solution.py:46
  24.1 10.3 %collective-permute-start.4 = (f32[19,1,10,130]{3,2,1,0:T(8,128)S(1)}, f32[19,1,10,130]{3,2,1,0:T(8,128)S(1)}, u32[]{:S(2)}, u32[]{:S(2)}) collective-permute-start(f32[19,1,10,130]{3,2,1,0:T(8,128)S(1)} %get-tuple-element.146), channel_id=1, source_target_pairs={{1,0},{0,1},{3,2},{2,3},{5,4},{4,5},{7,6},{6,7},{9,8},{8,9},{11,10... | collective-permute-start | bytes 296408 | tf_op jit(solution)/shard_map/ppermute | solution.py:47
  25.7 14.9 %collective-permute-start.5 = (f32[19,1,10,130]{3,2,1,0:T(8,128)S(1)}, f32[19,1,10,130]{3,2,1,0:T(8,128)S(1)}, u32[]{:S(2)}, u32[]{:S(2)}) collective-permute-start(f32[19,1,10,130]{3,2,1,0:T(8,128)S(1)} %get-tuple-element.145), channel_id=1, source_target_pairs={{0,1},{1,0},{2,3},{3,2},{4,5},{5,4},{6,7},{7,6},{8,9},{9,8},{10,11... | collective-permute-start | bytes 296408 | tf_op jit(solution)/shard_map/ppermute | solution.py:46
  42.2 4.5 %collective-permute-start.6 = (f32[19,8,1,128]{3,2,1,0:T(1,128)S(1)}, f32[19,8,1,128]{3,2,1,0:T(1,128)S(1)}, u32[]{:S(2)}, u32[]{:S(2)}) collective-permute-start(f32[19,8,1,128]{3,2,1,0:T(1,128)S(1)} %get-tuple-element.160), channel_id=1, source_target_pairs={{8,0},{16,8},{24,16},{0,24},{9,1},{17,9},{25,17},{1,25},{10,2},{18... | collective-permute-start | bytes 233480 | tf_op jit(solution)/shard_map/ppermute | solution.py:47
  42.8 6.2 %collective-permute-start.7 = (f32[19,8,1,128]{3,2,1,0:T(1,128)S(1)}, f32[19,8,1,128]{3,2,1,0:T(1,128)S(1)}, u32[]{:S(2)}, u32[]{:S(2)}) collective-permute-start(f32[19,8,1,128]{3,2,1,0:T(1,128)S(1)} %get-tuple-element.159), channel_id=1, source_target_pairs={{0,8},{8,16},{16,24},{24,0},{1,9},{9,17},{17,25},{25,1},{2,10},{10... | collective-permute-start | bytes 233480 | tf_op jit(solution)/shard_map/ppermute | solution.py:46
  50.4 1.7 collective-permute-start.8
  51.1 3.6 %collective-permute-start.9 = (f32[19,8,10,1]{0,1,3,2:T(8,128)S(1)}, f32[19,8,10,1]{0,1,3,2:T(8,128)S(1)}, u32[]{:S(2)}, u32[]{:S(2)}) collective-permute-start(f32[19,8,10,1]{0,1,3,2:T(8,128)S(1)} %copy.208), channel_id=1, source_target_pairs={{0,2},{2,4},{4,6},{6,0},{1,3},{3,5},{5,7},{7,1},{8,10},{10,12},{12... | collective-permute-start | bytes 18248 | tf_op jit(solution)/shard_map/ppermute | solution.py:46
  56.6 10.3 %collective-permute-start.10 = (f32[19,1,10,130]{3,2,1,0:T(8,128)S(1)}, f32[19,1,10,130]{3,2,1,0:T(8,128)S(1)}, u32[]{:S(2)}, u32[]{:S(2)}) collective-permute-start(f32[19,1,10,130]{3,2,1,0:T(8,128)S(1)} %get-tuple-element.144), channel_id=1, source_target_pairs={{1,0},{0,1},{3,2},{2,3},{5,4},{4,5},{7,6},{6,7},{9,8},{8,9},{11,10... | collective-permute-start | bytes 296408 | tf_op jit(solution)/shard_map/ppermute | solution.py:47
  58.2 13.8 %collective-permute-start.11 = (f32[19,1,10,130]{3,2,1,0:T(8,128)S(1)}, f32[19,1,10,130]{3,2,1,0:T(8,128)S(1)}, u32[]{:S(2)}, u32[]{:S(2)}) collective-permute-start(f32[19,1,10,130]{3,2,1,0:T(8,128)S(1)} %get-tuple-element.143), channel_id=1, source_target_pairs={{0,1},{1,0},{2,3},{3,2},{4,5},{5,4},{6,7},{7,6},{8,9},{9,8},{10,11... | collective-permute-start | bytes 296408 | tf_op jit(solution)/shard_map/ppermute | solution.py:46
  73.5 31.1 %copy-start = (f32[19,8,8,128]{3,2,1,0:T(8,128)}, f32[19,8,8,128]{3,2,1,0:T(8,128)S(1)}, u32[]{:S(2)}) copy-start(f32[19,8,8,128]{3,2,1,0:T(8,128)S(1)} %add_select_fusion.1) | copy-start | bytes 1867780
  73.6 4.8 %collective-permute-start.12 = (f32[19,8,1,128]{3,2,1,0:T(1,128)S(1)}, f32[19,8,1,128]{3,2,1,0:T(1,128)S(1)}, u32[]{:S(2)}, u32[]{:S(2)}) collective-permute-start(f32[19,8,1,128]{3,2,1,0:T(1,128)S(1)} %get-tuple-element.158), channel_id=1, source_target_pairs={{8,0},{16,8},{24,16},{0,24},{9,1},{17,9},{25,17},{1,25},{10,2},{18... | collective-permute-start | bytes 233480 | tf_op jit(solution)/shard_map/ppermute | solution.py:47
  73.8 6.2 %collective-permute-start.13 = (f32[19,8,1,128]{3,2,1,0:T(1,128)S(1)}, f32[19,8,1,128]{3,2,1,0:T(1,128)S(1)}, u32[]{:S(2)}, u32[]{:S(2)}) collective-permute-start(f32[19,8,1,128]{3,2,1,0:T(1,128)S(1)} %get-tuple-element.157), channel_id=1, source_target_pairs={{0,8},{8,16},{16,24},{24,0},{1,9},{9,17},{17,25},{25,1},{2,10},{10... | collective-permute-start | bytes 233480 | tf_op jit(solution)/shard_map/ppermute | solution.py:46
  81.3 1.7 collective-permute-start.14
  82.1 3.9 %collective-permute-start.15 = (f32[19,8,10,1]{0,1,3,2:T(8,128)S(1)}, f32[19,8,10,1]{0,1,3,2:T(8,128)S(1)}, u32[]{:S(2)}, u32[]{:S(2)}) collective-permute-start(f32[19,8,10,1]{0,1,3,2:T(8,128)S(1)} %copy.214), channel_id=1, source_target_pairs={{0,2},{2,4},{4,6},{6,0},{1,3},{3,5},{5,7},{7,1},{8,10},{10,12},{12... | collective-permute-start | bytes 18248 | tf_op jit(solution)/shard_map/ppermute | solution.py:46
  87.9 16.7 %copy-start.25 = (f32[19,8,1,128]{3,2,1,0:T(1,128)S(1)}, f32[19,8,1,128]{3,2,1,0:T(1,128)}, u32[]{:S(2)}) copy-start(f32[19,8,1,128]{3,2,1,0:T(1,128)} %copy-done.24) | copy-start | bytes 233476
  87.9 16.7 %copy-start.27 = (f32[19,8,1,128]{3,2,1,0:T(1,128)S(1)}, f32[19,8,1,128]{3,2,1,0:T(1,128)}, u32[]{:S(2)}) copy-start(f32[19,8,1,128]{3,2,1,0:T(1,128)} %copy-done.26) | copy-start | bytes 233476
  87.9 10.3 %collective-permute-start.16 = (f32[19,1,10,130]{3,2,1,0:T(8,128)S(1)}, f32[19,1,10,130]{3,2,1,0:T(8,128)S(1)}, u32[]{:S(2)}, u32[]{:S(2)}) collective-permute-start(f32[19,1,10,130]{3,2,1,0:T(8,128)S(1)} %get-tuple-element.142), channel_id=1, source_target_pairs={{1,0},{0,1},{3,2},{2,3},{5,4},{4,5},{7,6},{6,7},{9,8},{8,9},{11,10... | collective-permute-start | bytes 296408 | tf_op jit(solution)/shard_map/ppermute | solution.py:47
  89.5 15.1 %collective-permute-start.17 = (f32[19,1,10,130]{3,2,1,0:T(8,128)S(1)}, f32[19,1,10,130]{3,2,1,0:T(8,128)S(1)}, u32[]{:S(2)}, u32[]{:S(2)}) collective-permute-start(f32[19,1,10,130]{3,2,1,0:T(8,128)S(1)} %get-tuple-element.141), channel_id=1, source_target_pairs={{0,1},{1,0},{2,3},{3,2},{4,5},{5,4},{6,7},{7,6},{8,9},{9,8},{10,11... | collective-permute-start | bytes 296408 | tf_op jit(solution)/shard_map/ppermute | solution.py:46
  106.8 6.7 %collective-permute-start.18 = (f32[19,8,1,128]{3,2,1,0:T(1,128)S(1)}, f32[19,8,1,128]{3,2,1,0:T(1,128)S(1)}, u32[]{:S(2)}, u32[]{:S(2)}) collective-permute-start(f32[19,8,1,128]{3,2,1,0:T(1,128)S(1)} %get-tuple-element.156), channel_id=1, source_target_pairs={{0,8},{8,16},{16,24},{24,0},{1,9},{9,17},{17,25},{25,1},{2,10},{10... | collective-permute-start | bytes 233480 | tf_op jit(solution)/shard_map/ppermute | solution.py:46
  106.9 6.7 %collective-permute-start.19 = (f32[19,8,1,128]{3,2,1,0:T(1,128)S(1)}, f32[19,8,1,128]{3,2,1,0:T(1,128)S(1)}, u32[]{:S(2)}, u32[]{:S(2)}) collective-permute-start(f32[19,8,1,128]{3,2,1,0:T(1,128)S(1)} %get-tuple-element.155), channel_id=1, source_target_pairs={{8,0},{16,8},{24,16},{0,24},{9,1},{17,9},{25,17},{1,25},{10,2},{18... | collective-permute-start | bytes 233480 | tf_op jit(solution)/shard_map/ppermute | solution.py:47
  115.6 3.9 %collective-permute-start.20 = (f32[19,8,10,1]{0,1,3,2:T(8,128)}, f32[19,8,10,1]{0,1,3,2:T(8,128)S(1)}, u32[]{:S(2)}, u32[]{:S(2)}) collective-permute-start(f32[19,8,10,1]{0,1,3,2:T(8,128)} %copy.218), channel_id=1, source_target_pairs={{0,2},{2,4},{4,6},{6,0},{1,3},{3,5},{5,7},{7,1},{8,10},{10,12},{12... | collective-permute-start | bytes 18248 | tf_op jit(solution)/shard_map/ppermute | solution.py:46
  116.3 4.5 %collective-permute-start.21 = (f32[19,8,10,1]{0,1,3,2:T(8,128)S(1)}, f32[19,8,10,1]{0,1,3,2:T(8,128)}, u32[]{:S(2)}, u32[]{:S(2)}) collective-permute-start(f32[19,8,10,1]{0,1,3,2:T(8,128)S(1)} %copy.220), channel_id=1, source_target_pairs={{2,0},{4,2},{6,4},{0,6},{3,1},{5,3},{7,5},{1,7},{10,8},{12,10},{14... | collective-permute-start | bytes 18248 | tf_op jit(solution)/shard_map/ppermute | solution.py:47
  122.9 15.3 %copy-start.7 = (f32[1,8,8,128]{3,2,1,0:T(8,128)S(1)}, f32[1,8,8,128]{3,2,1,0:T(8,128)}, u32[]{:S(2)}) copy-start(f32[1,8,8,128]{3,2,1,0:T(8,128)} %copy-done.6) | copy-start | bytes 98308
  122.9 15.3 %copy-start.9 = (f32[1,8,8,128]{3,2,1,0:T(8,128)S(1)}, f32[1,8,8,128]{3,2,1,0:T(8,128)}, u32[]{:S(2)}) copy-start(f32[1,8,8,128]{3,2,1,0:T(8,128)} %copy-done.8) | copy-start | bytes 98308
  123.0 15.3 %copy-start.11 = (f32[1,8,8,128]{3,2,1,0:T(8,128)S(1)}, f32[1,8,8,128]{3,2,1,0:T(8,128)}, u32[]{:S(2)}) copy-start(f32[1,8,8,128]{3,2,1,0:T(8,128)} %copy-done.10) | copy-start | bytes 98308
  123.0 15.3 %copy-start.15 = (f32[1,8,8,128]{3,2,1,0:T(8,128)S(1)}, f32[1,8,8,128]{3,2,1,0:T(8,128)}, u32[]{:S(2)}) copy-start(f32[1,8,8,128]{3,2,1,0:T(8,128)} %copy-done.14) | copy-start | bytes 98308
  123.0 15.3 %copy-start.21 = (f32[1,8,8,128]{3,2,1,0:T(8,128)S(1)}, f32[1,8,8,128]{3,2,1,0:T(8,128)}, u32[]{:S(2)}) copy-start(f32[1,8,8,128]{3,2,1,0:T(8,128)} %copy-done.20) | copy-start | bytes 98308
  123.5 10.3 %collective-permute-start.22 = (f32[19,1,10,130]{3,2,1,0:T(8,128)S(1)}, f32[19,1,10,130]{3,2,1,0:T(8,128)S(1)}, u32[]{:S(2)}, u32[]{:S(2)}) collective-permute-start(f32[19,1,10,130]{3,2,1,0:T(8,128)S(1)} %get-tuple-element.139), channel_id=1, source_target_pairs={{0,1},{1,0},{2,3},{3,2},{4,5},{5,4},{6,7},{7,6},{8,9},{9,8},{10,11... | collective-permute-start | bytes 296408 | tf_op jit(solution)/shard_map/ppermute | solution.py:46
  125.1 13.1 %collective-permute-start.23 = (f32[19,1,10,130]{3,2,1,0:T(8,128)S(1)}, f32[19,1,10,130]{3,2,1,0:T(8,128)S(1)}, u32[]{:S(2)}, u32[]{:S(2)}) collective-permute-start(f32[19,1,10,130]{3,2,1,0:T(8,128)S(1)} %get-tuple-element.140), channel_id=1, source_target_pairs={{1,0},{0,1},{3,2},{2,3},{5,4},{4,5},{7,6},{6,7},{9,8},{8,9},{11,10... | collective-permute-start | bytes 296408 | tf_op jit(solution)/shard_map/ppermute | solution.py:47
  (48 other events, 166.3 us)
